TPU v7x, 32 devices: a whole 2x2x4 slice. The times are simulated.
32 devices in a mesh: groups: 2 (over y), expert: 4 (over z), tensor: 2 (over x), sub: 2 (over core).
Axes of the slice: x: 2, y: 2, z: 4, core: 2. Of those that a mesh axis runs over, the one named last changes fastest.
Arguments:
- tokens: bfloat16 [48, 7168], P(('groups', 'expert', 'tensor'), 'sub'), parts along dimension 0, may hold values from -6 to 6
- expert_ids: int32 [48, 8], P(('groups', 'expert', 'tensor')), parts along dimension 0, may hold values from 0 to 15, all different within a row; in each aligned block of 3 rows (0 to 2, 3 to 5, ...) at most 2 rows name the same one
- gate_weights: float32 [48, 8], P(('groups', 'expert', 'tensor')), parts along dimension 0, may hold values from 0.1 to 0.6
- gate_proj: bfloat16 [16, 1024, 7168], P('expert', 'tensor', 'sub'), may hold values from -0.0625 to 0.0625
- up_proj: bfloat16 [16, 1024, 7168], P('expert', 'tensor', 'sub'), may hold values from -0.0625 to 0.0625
- down_proj: bfloat16 [16, 1024, 7168], P('expert', 'tensor', 'sub'), may hold values from -0.1875 to 0.1875
Outputs:
- blended: bfloat16 [48, 7168], P(('groups', 'expert', 'tensor'), 'sub'), parts along dimension 0
There are 2 independent parts, one for each index of `groups`. A program takes and returns all parts, laid end to end along the dimension named above; an argument that names none is the same for every part. Nothing has to cross between parts.
Inputs may be any that keep to these rules, and one draw needn't show every extreme that they name: `expert_ids`: each row names 8 different experts. Among the rows of one owner (aligned blocks of 3 rows) no expert is named by more than 2 rows, a bound that some block reaches.
All inputs are finite; a program needn't handle non-finite values.
Results may differ from a plain program's by a relative error of at most 0.02.
Values may be sent and summed in bfloat16 or wider, within the bound.
A program may use at most 128 MiB of HBM per device.

v0:
```python
import jax
import jax.numpy as jnp
from jax import lax
from jax.sharding import PartitionSpec as P

SLOTS = 2


def per_device(tokens, expert_ids, gate_weights, gate_proj, up_proj, down_proj):
    expert_count = lax.axis_size("expert")
    tensor_count = lax.axis_size("tensor")
    local_count = gate_proj.shape[0]
    total_experts = expert_count * local_count
    features = tokens.shape[1]
    owned = tokens.shape[0]
    labels = jnp.arange(total_experts, dtype=jnp.int32)
    chosen = expert_ids[:, :, None] == labels[None, None, :]
    picked = jnp.sum(chosen.astype(jnp.int32), axis=1)
    before = jnp.cumsum(picked, axis=0) - picked
    slot_ids = jnp.arange(SLOTS, dtype=jnp.int32)
    placed = (picked[:, :, None] == 1) & (before[:, :, None] == slot_ids[None, None, :])
    placed_flat = placed.reshape(owned, total_experts * SLOTS)
    outgoing = jnp.dot(
        placed_flat.astype(jnp.bfloat16).T, tokens, preferred_element_type=jnp.float32
    ).astype(jnp.bfloat16)
    slab = local_count * SLOTS * features
    outgoing = outgoing.reshape(expert_count, slab)
    peers = expert_count * tensor_count
    copies = jnp.broadcast_to(outgoing[:, None, :], (expert_count, tensor_count, slab)).reshape(
        peers, slab
    )
    arrived = lax.all_to_all(copies, ("expert", "tensor"), split_axis=0, concat_axis=0, tiled=True)
    rows_in = jnp.moveaxis(arrived.reshape(peers, local_count, SLOTS, features), 1, 0)
    rows_in = rows_in.reshape(local_count, peers * SLOTS, features)
    gate_part = jnp.einsum("lrd,lfd->lrf", rows_in, gate_proj, preferred_element_type=jnp.float32)
    up_part = jnp.einsum("lrd,lfd->lrf", rows_in, up_proj, preferred_element_type=jnp.float32)
    gate_full, up_full = (
        lax.psum(gate_part.astype(jnp.bfloat16), "sub").astype(jnp.float32),
        lax.psum(up_part.astype(jnp.bfloat16), "sub").astype(jnp.float32),
    )
    hidden = (jax.nn.silu(gate_full) * up_full).astype(jnp.bfloat16)
    partial_value = jnp.einsum(
        "lrf,lfd->lrd", hidden, down_proj, preferred_element_type=jnp.float32
    ).astype(jnp.bfloat16)
    partial_value = jnp.moveaxis(
        partial_value.reshape(local_count, peers, SLOTS, features), 0, 1
    ).reshape(peers, slab)
    returned = lax.all_to_all(
        partial_value, ("expert", "tensor"), split_axis=0, concat_axis=0, tiled=True
    )
    returned = returned.reshape(expert_count, tensor_count, slab)
    results = jnp.sum(returned.astype(jnp.float32), axis=1).reshape(total_experts * SLOTS, features)
    weight_table = jnp.sum(gate_weights[:, :, None] * chosen.astype(jnp.float32), axis=1)
    mixing = (weight_table[:, :, None] * placed.astype(jnp.float32)).reshape(
        owned, total_experts * SLOTS
    )
    blended = jnp.dot(mixing, results, precision=lax.Precision.HIGHEST)
    return blended.astype(jnp.bfloat16)


def solution(mesh):
    placed = (
        P(("groups", "expert", "tensor"), "sub"),
        P(("groups", "expert", "tensor"), None),
        P(("groups", "expert", "tensor"), None),
        P("expert", "tensor", "sub"),
        P("expert", "tensor", "sub"),
        P("expert", "tensor", "sub"),
    )
    return jax.shard_map(
        per_device,
        mesh=mesh,
        in_specs=placed,
        out_specs=P(("groups", "expert", "tensor"), "sub"),
        check_vma=False,
    )
```

profile of v0, /device:TPU:0, one launch (start us, length us, event | category | flops | bytes accessed | tf_op | source)
XLA Modules:
  0.0 119.9 jit_solution(9019192052215831962)
XLA Ops:
  6.5 0.8 convert_reduce_fusion.1
  8.5 0.5 all_to_all.16
  9.0 0.5 broadcast.69
  9.5 3.5 %reduce.3 = bf16[8,28672]{1,0:T(8,128)(2,1)S(1)} reduce(bf16[8,1,28672]{2,1,0:T(2,128)(2,1)S(1)} %all_to_all.16, bf16[]{:T(256)} %broadcast.69), dimensions={1}, to_apply=%all_to_all.16.reduce_sub_computation | reduce | bytes 917506 | tf_op jit(solution)/shard_map/all_to_all | solution.py:32
  13.0 0.3 reshape.94
  13.4 20.3 %all_to_all.20 = bf16[8,2,14336]{2,1,0:T(2,128)(2,1)S(1)} all-to-all(bf16[8,2,14336]{2,1,0:T(2,128)(2,1)S(1)} %reshape.94), channel_id=1, replica_groups=mesh['groups'=2,'expert'=4,'tensor'=2,'sub'=2] {'expert','tensor'}, dimensions={0} | all-to-all | bytes 917504 | tf_op jit(solution)/shard_map/all_to_all | solution.py:32
  33.7 0.5 reshape.95
  34.1 2.9 %reduce = bf16[8,28672]{1,0:T(8,128)(2,1)S(1)} reduce(bf16[8,1,28672]{2,1,0:T(2,128)(2,1)S(1)} %reshape.95, bf16[]{:T(256)} %constant.17), dimensions={1}, to_apply=%all_to_all.13.reduce_sub_computation | reduce | bytes 917506 | tf_op jit(solution)/shard_map/all_to_all | solution.py:32
  37.0 0.3 reshape.87
  37.9 9.7 %convolution_convert_fusion.3 = bf16[4,16,512]{2,1,0:T(8,128)(2,1)} fusion(bf16[4,16,3584]{2,1,0:T(8,128)(2,1)S(1)} %reshape.88, bf16[4,512,3584]{2,1,0:T(8,128)(2,1)} %param.10), kind=kOutput, calls=%fused_computation.3 | convolution fusion | flops 234913792 | bytes 15204352 | tf_op jit(solution)/shard_map/lrd,lfd->lrf/dot_general | solution.py:36
  47.5 9.7 %convolution_convert_fusion.4 = bf16[4,16,512]{2,1,0:T(8,128)(2,1)} fusion(bf16[4,16,3584]{2,1,0:T(8,128)(2,1)S(1)} %reshape.88, bf16[4,512,3584]{2,1,0:T(8,128)(2,1)} %param.9), kind=kOutput, calls=%fused_computation.4 | convolution fusion | flops 234913792 | bytes 15204352 | tf_op jit(solution)/shard_map/lrd,lfd->lrf/dot_general | solution.py:35
  57.3 17.1 %all-reduce.3.cloned.1.call-done = (bf16[4,16,512]{2,1,0:T(8,128)(2,1)}, bf16[4,16,512]{2,1,0:T(8,128)(2,1)}) async-done(((bf16[4,16,512]{2,1,0:T(8,128)(2,1)}, bf16[4,16,512]{2,1,0:T(8,128)(2,1)}), (bf16[4,16,512]{2,1,0:T(8,128)(2,1)}, bf16[4,16,512]{2,1,0:T(8,128)(2,1)})) %all-reduce.3.cloned.1.call-update) | async-done | bytes 131088 | tf_op jit(solution)/shard_map/psum | solution.py:39
  74.4 7.3 %convolution_convert_fusion = bf16[4,16,3584]{2,1,0:T(8,128)(2,1)S(1)} fusion(bf16[4,512,3584]{2,1,0:T(8,128)(2,1)} %param.11, bf16[4,16,512]{2,1,0:T(8,128)(2,1)} %get-tuple-element.5, bf16[4,16,512]{2,1,0:T(8,128)(2,1)} %get-tuple-element.6), kind=kOutput, calls=%fused_computation | convolution fusion | flops 235372544 | bytes 15269888 | tf_op jit(solution)/shard_map/lrf,lfd->lrd/dot_general | solution.py:42
  82.1 0.6 all_to_all.17
  82.8 3.5 %reduce.4 = bf16[8,28672]{1,0:T(8,128)(2,1)S(1)} reduce(bf16[8,1,28672]{2,1,0:T(2,128)(2,1)S(1)} %all_to_all.17, bf16[]{:T(256)} %broadcast.69), dimensions={1}, to_apply=%all_to_all.17.reduce_sub_computation | reduce | bytes 917506 | tf_op jit(solution)/shard_map/all_to_all | solution.py:48
  86.3 1.1 reshape.96
  87.4 5.8 %all-to-all-start.1 = ((bf16[8,2,14336]{2,1,0:T(2,128)(2,1)}), bf16[8,2,14336]{2,1,0:T(2,128)(2,1)S(1)}, u32[]{:S(2)}, u32[]{:S(2)}) async-start(bf16[8,2,14336]{2,1,0:T(2,128)(2,1)} %reshape.96), calls=%async_computation.1 | async-start | bytes 917504 | tf_op jit(solution)/shard_map/all_to_all | solution.py:48
  93.5 13.2 %all-to-all-done.1 = bf16[8,2,14336]{2,1,0:T(2,128)(2,1)S(1)} async-done(((bf16[8,2,14336]{2,1,0:T(2,128)(2,1)}), bf16[8,2,14336]{2,1,0:T(2,128)(2,1)S(1)}, u32[]{:S(2)}, u32[]{:S(2)}) %all-to-all-start.1) | async-done | bytes 458784 | tf_op jit(solution)/shard_map/all_to_all | solution.py:48
  106.7 0.5 reshape.97
  107.2 2.7 %convert_reduce_fusion = f32[8,28672]{1,0:T(8,128)S(1)} fusion(bf16[8,1,28672]{2,1,0:T(2,128)(2,1)S(1)} %reshape.97), kind=kLoop, calls=%fused_computation.5 | loop fusion | flops 229376 | bytes 1376256 | tf_op jit(solution)/shard_map/convert_element_type | solution.py:52
  109.9 0.5 reshape.91
  110.4 1.3 %reduce_sum.29 = f32[4,28672]{1,0:T(4,128)S(1)} reduce(f32[4,2,28672]{2,1,0:T(2,128)S(1)} %reshape.91, f32[]{:T(128)} %constant.12.clone.1), dimensions={1}, to_apply=%region_5.6 | reduce | flops 114688 | bytes 1376260 | tf_op jit(solution)/shard_map/reduce_sum | solution.py:52
  111.7 0.3 reshape.90
  112.1 0.9 convolution_convert_fusion.2
  (27 shorter events, 2.4 us)
Async XLA Ops:
  6.5 1.3 %copy-start = (bf16[3,3584]{1,0:T(4,128)(2,1)S(1)}, bf16[3,3584]{1,0:T(4,128)(2,1)}, u32[]{:S(2)}) copy-start(bf16[3,3584]{1,0:T(4,128)(2,1)} %param.6) | copy-start | bytes 64516
  6.5 67.8 %all-reduce.3.cloned.1.call-start = ((), (), s32[]{:S(2)}) async-start(), calls=%async_computation.2 | async-start | bytes 262144 | tf_op jit(solution)/shard_map/psum | solution.py:39
  57.2 36.0 %copy-start.1 = (s32[3,8]{1,0:T(4,128)S(1)}, s32[3,8]{1,0:T(4,128)}, u32[]{:S(2)}) copy-start(s32[3,8]{1,0:T(4,128)} %param.7) | copy-start | bytes 292
  57.2 36.0 %copy-start.2 = (f32[3,8]{1,0:T(4,128)S(1)}, f32[3,8]{1,0:T(4,128)}, u32[]{:S(2)}) copy-start(f32[3,8]{1,0:T(4,128)} %param.8) | copy-start | bytes 292
  87.4 19.3 %all-to-all-start.1 = ((bf16[8,2,14336]{2,1,0:T(2,128)(2,1)}), bf16[8,2,14336]{2,1,0:T(2,128)(2,1)S(1)}, u32[]{:S(2)}, u32[]{:S(2)}) async-start(bf16[8,2,14336]{2,1,0:T(2,128)(2,1)} %reshape.96), calls=%async_computation.1 | async-start | bytes 917504 | tf_op jit(solution)/shard_map/all_to_all | solution.py:48
Sparse Core Ops, SparseCore 0:
  57.4 16.9 all-reduce.2
where the time goes:
time: 120 us
  waiting for transfers between devices  30.3 us (25%)
  matrix products  27.8 us (23%)
  blocking collectives  20.3 us (17%)
  other arithmetic  15 us (12%)
  between operations  13.6 us (11%)
  local copies, waits for them, and re-layouts  7.07 us (6%)
  starting transfers between devices  5.82 us (5%)
    all_to_all x1, blocking collectives, per_device(): lax.all_to_all(copies, ('expert', 'tensor'), split_axis=0, concat_axis=0,...  20.3 us
    psum x1, waiting for transfers between devices, per_device(): lax.psum(up_part.astype(jnp.bfloat16), 'sub').astype(jnp.float32)  17.1 us
    all_to_all x1, waiting for transfers between devices, per_device(): lax.all_to_all(partial_value, ('expert', 'tensor'), split_axis=0, concat_...  13.2 us
    dot_general x1, matrix products, per_device(): jnp.einsum('lrd,lfd->lrf', rows_in, up_proj, preferred_element_type=jnp.f...  9.69 us
    dot_general x1, matrix products, per_device(): jnp.einsum('lrd,lfd->lrf', rows_in, gate_proj, preferred_element_type=jnp...  9.68 us
    dot_general x1, matrix products, per_device(): jnp.einsum('lrf,lfd->lrd', hidden, down_proj, preferred_element_type=jnp....  7.26 us
    all_to_all x2, other arithmetic, per_device(): lax.all_to_all(copies, ('expert', 'tensor'), split_axis=0, concat_axis=0,...  6.41 us
    all_to_all x1, starting transfers between devices, per_device(): lax.all_to_all(partial_value, ('expert', 'tensor'), split_axis=0, concat_...  5.81 us
  transfers between devices with their start and end apart: 2, of which 2 were waited for; matrix products, arithmetic and copies ran while one was open for 0% of the time, Pallas kernels for 0%

commit v1 on v0

--- a/solution.py
+++ b/solution.py
@@ -4,6 +4,12 @@
 from jax.sharding import PartitionSpec as P
 
 SLOTS = 2
+
+
+def gather_and_add(block, axis):
+    terms = lax.all_gather(block, axis, axis=0, tiled=False)
+    total = terms.sum(axis=0)
+    return total
 
 
 def per_device(tokens, expert_ids, gate_weights, gate_proj, up_proj, down_proj):
@@ -36,7 +42,7 @@
     up_part = jnp.einsum("lrd,lfd->lrf", rows_in, up_proj, preferred_element_type=jnp.float32)
     gate_full, up_full = (
         lax.psum(gate_part.astype(jnp.bfloat16), "sub").astype(jnp.float32),
-        lax.psum(up_part.astype(jnp.bfloat16), "sub").astype(jnp.float32),
+        gather_and_add(up_part.astype(jnp.bfloat16), "sub").astype(jnp.float32),
     )
     hidden = (jax.nn.silu(gate_full) * up_full).astype(jnp.bfloat16)
     partial_value = jnp.einsum(

time: 120 us -> 110 us (0.917)
  waiting for transfers between devices: 30.3 us -> 18.8 us
  blocking collectives: 20.3 us -> 22.5 us
    psum x1, waiting for transfers between devices: 17.1 us -> 5.54 us  [per_device(): lax.psum(gate_part.astype(jnp.bfloat16), 'sub').astype(jnp.float32)]
    all_gather x0 -> x1, blocking collectives: none -> 2.2 us  [gather_and_add(): terms = lax.all_gather(block, axis, axis=0, tiled=False)]
  transfers between devices with their start and end apart: 2 -> 2, of which waited for: 2 -> 2; matrix products, arithmetic and copies ran while one was open for 0% -> 9% of each run, Pallas kernels for 0% -> 0%
where the time goes in v1:
time: 110 us
  matrix products  27.2 us (25%)
  blocking collectives  22.5 us (20%)
  waiting for transfers between devices  18.8 us (17%)
  other arithmetic  15 us (14%)
  between operations  13.6 us (12%)
  local copies, waits for them, and re-layouts  6.85 us (6%)
  starting transfers between devices  5.82 us (5%)
    all_to_all x1, blocking collectives, per_device(): lax.all_to_all(copies, ('expert', 'tensor'), split_axis=0, concat_axis=0,...  20.3 us
    all_to_all x1, waiting for transfers between devices, per_device(): lax.all_to_all(partial_value, ('expert', 'tensor'), split_axis=0, concat_...  13.2 us
    dot_general x1, matrix products, per_device(): jnp.einsum('lrd,lfd->lrf', rows_in, gate_proj, preferred_element_type=jnp...  9.69 us
    dot_general x1, matrix products, per_device(): jnp.einsum('lrd,lfd->lrf', rows_in, up_proj, preferred_element_type=jnp.f...  9.07 us
    dot_general x1, matrix products, per_device(): jnp.einsum('lrf,lfd->lrd', hidden, down_proj, preferred_element_type=jnp....  7.22 us
    all_to_all x2, other arithmetic, per_device(): lax.all_to_all(copies, ('expert', 'tensor'), split_axis=0, concat_axis=0,...  6.41 us
    all_to_all x1, starting transfers between devices, per_device(): lax.all_to_all(partial_value, ('expert', 'tensor'), split_axis=0, concat_...  5.81 us
    psum x1, waiting for transfers between devices, per_device(): lax.psum(gate_part.astype(jnp.bfloat16), 'sub').astype(jnp.float32)  5.54 us
  transfers between devices with their start and end apart: 2, of which 2 were waited for; matrix products, arithmetic and copies ran while one was open for 9% of the time, Pallas kernels for 0%

profile of v1, /device:TPU:0, one launch (start us, length us, event | category | flops | bytes accessed | tf_op | source)
XLA Modules:
  0.0 109.7 jit_solution(14223483174865200396)
XLA Ops:
  6.5 0.8 convert_reduce_fusion.1
  8.5 0.5 all_to_all.16
  9.0 0.5 broadcast.69
  9.5 3.5 %reduce.4 = bf16[8,28672]{1,0:T(8,128)(2,1)S(1)} reduce(bf16[8,1,28672]{2,1,0:T(2,128)(2,1)S(1)} %all_to_all.16, bf16[]{:T(256)} %broadcast.69), dimensions={1}, to_apply=%all_to_all.16.reduce_sub_computation | reduce | bytes 917506 | tf_op jit(solution)/shard_map/all_to_all | solution.py:38
  13.0 0.3 reshape.95
  13.4 20.3 %all_to_all.20 = bf16[8,2,14336]{2,1,0:T(2,128)(2,1)S(1)} all-to-all(bf16[8,2,14336]{2,1,0:T(2,128)(2,1)S(1)} %reshape.95), channel_id=1, replica_groups=mesh['groups'=2,'expert'=4,'tensor'=2,'sub'=2] {'expert','tensor'}, dimensions={0} | all-to-all | bytes 917504 | tf_op jit(solution)/shard_map/all_to_all | solution.py:38
  33.7 0.5 reshape.96
  34.1 2.9 %reduce.1 = bf16[8,28672]{1,0:T(8,128)(2,1)S(1)} reduce(bf16[8,1,28672]{2,1,0:T(2,128)(2,1)S(1)} %reshape.96, bf16[]{:T(256)} %constant.19), dimensions={1}, to_apply=%all_to_all.13.reduce_sub_computation | reduce | bytes 917506 | tf_op jit(solution)/shard_map/all_to_all | solution.py:38
  37.0 0.3 reshape.87
  37.9 9.7 %convolution_convert_fusion.4 = bf16[4,16,512]{2,1,0:T(8,128)(2,1)} fusion(bf16[4,16,3584]{2,1,0:T(8,128)(2,1)S(1)} %reshape.88, bf16[4,512,3584]{2,1,0:T(8,128)(2,1)} %param.9), kind=kOutput, calls=%fused_computation.4 | convolution fusion | flops 234913792 | bytes 15204352 | tf_op jit(solution)/shard_map/lrd,lfd->lrf/dot_general | solution.py:41
  47.6 9.1 %convolution_convert_fusion.3 = bf16[4,16,512]{2,1,0:T(8,128)(2,1)S(1)} fusion(bf16[4,16,3584]{2,1,0:T(8,128)(2,1)S(1)} %reshape.88, bf16[4,512,3584]{2,1,0:T(8,128)(2,1)} %param.10), kind=kOutput, calls=%fused_computation.3 | convolution fusion | flops 234913792 | bytes 15204352 | tf_op jit(solution)/shard_map/lrd,lfd->lrf/dot_general | solution.py:42
  56.6 2.2 %all-gather = bf16[8,16,512]{2,1,0:T(8,128)(2,1)S(1)} all-gather(bf16[4,16,512]{2,1,0:T(8,128)(2,1)S(1)} %convolution_convert_fusion.3), channel_id=2, replica_groups=mesh['groups'=2,'expert'=4,'tensor'=2,'sub'=2] {'sub'}, dimensions={0}, use_global_device_ids=true | all-gather | bytes 196608 | tf_op jit(solution)/shard_map/all_gather | solution.py:10
  58.9 5.5 %all-reduce.2.cloned.1.call-done = bf16[4,16,512]{2,1,0:T(8,128)(2,1)} async-done(((bf16[4,16,512]{2,1,0:T(8,128)(2,1)}), bf16[4,16,512]{2,1,0:T(8,128)(2,1)}) %all-reduce.2.cloned.1.call-update) | async-done | bytes 65552 | tf_op jit(solution)/shard_map/psum | solution.py:44
  64.4 7.2 %convolution_convert_fusion = bf16[4,16,3584]{2,1,0:T(8,128)(2,1)S(1)} fusion(bf16[4,512,3584]{2,1,0:T(8,128)(2,1)} %param.11, bf16[4,16,512]{2,1,0:T(8,128)(2,1)S(1)} %reduce_sum.41, bf16[4,16,512]{2,1,0:T(8,128)(2,1)} %all-reduce.2.cloned.1.call-done), kind=kOutput, calls=%fused_computation | convolution fusion | flops 235372544 | bytes 15269888 | tf_op jit(solution)/shard_map/lrf,lfd->lrd/dot_general | solution.py:48
  72.2 0.4 all_to_all.17
  72.5 3.5 %reduce.5 = bf16[8,28672]{1,0:T(8,128)(2,1)S(1)} reduce(bf16[8,1,28672]{2,1,0:T(2,128)(2,1)S(1)} %all_to_all.17, bf16[]{:T(256)} %broadcast.69), dimensions={1}, to_apply=%all_to_all.17.reduce_sub_computation | reduce | bytes 917506 | tf_op jit(solution)/shard_map/all_to_all | solution.py:54
  76.1 1.1 %reshape.97 = bf16[8,2,14336]{2,1,0:T(2,128)(2,1)} reshape(bf16[8,28672]{1,0:T(8,128)(2,1)S(1)} %reduce.5) | data formatting | bytes 917504
  77.2 5.8 %all-to-all-start.1 = ((bf16[8,2,14336]{2,1,0:T(2,128)(2,1)}), bf16[8,2,14336]{2,1,0:T(2,128)(2,1)S(1)}, u32[]{:S(2)}, u32[]{:S(2)}) async-start(bf16[8,2,14336]{2,1,0:T(2,128)(2,1)} %reshape.97), calls=%async_computation.1 | async-start | bytes 917504 | tf_op jit(solution)/shard_map/all_to_all | solution.py:54
  83.3 13.2 %all-to-all-done.1 = bf16[8,2,14336]{2,1,0:T(2,128)(2,1)S(1)} async-done(((bf16[8,2,14336]{2,1,0:T(2,128)(2,1)}), bf16[8,2,14336]{2,1,0:T(2,128)(2,1)S(1)}, u32[]{:S(2)}, u32[]{:S(2)}) %all-to-all-start.1) | async-done | bytes 458784 | tf_op jit(solution)/shard_map/all_to_all | solution.py:54
  96.5 0.5 reshape.98
  97.0 2.7 %convert_reduce_fusion = f32[8,28672]{1,0:T(8,128)S(1)} fusion(bf16[8,1,28672]{2,1,0:T(2,128)(2,1)S(1)} %reshape.98), kind=kLoop, calls=%fused_computation.5 | loop fusion | flops 229376 | bytes 1376256 | tf_op jit(solution)/shard_map/convert_element_type | solution.py:58
  99.7 0.5 reshape.91
  100.2 1.3 %reduce_sum.42 = f32[4,28672]{1,0:T(4,128)S(1)} reduce(f32[4,2,28672]{2,1,0:T(2,128)S(1)} %reshape.91, f32[]{:T(128)} %constant.13.clone.1), dimensions={1}, to_apply=%region_5.6 | reduce | flops 114688 | bytes 1376260 | tf_op jit(solution)/shard_map/reduce_sum | solution.py:58
  101.9 0.9 convolution_convert_fusion.2
  (29 shorter events, 2.8 us)
Async XLA Ops:
  6.5 1.3 %copy-start = (bf16[3,3584]{1,0:T(4,128)(2,1)S(1)}, bf16[3,3584]{1,0:T(4,128)(2,1)}, u32[]{:S(2)}) copy-start(bf16[3,3584]{1,0:T(4,128)(2,1)} %param.6) | copy-start | bytes 64516
  6.5 57.9 %all-reduce.2.cloned.1.call-start = ((), (), s32[]{:S(2)}) async-start(), calls=%async_computation.2 | async-start | bytes 131072 | tf_op jit(solution)/shard_map/psum | solution.py:44
  56.6 26.4 %copy-start.1 = (s32[3,8]{1,0:T(4,128)S(1)}, s32[3,8]{1,0:T(4,128)}, u32[]{:S(2)}) copy-start(s32[3,8]{1,0:T(4,128)} %param.7) | copy-start | bytes 292
  56.6 26.4 %copy-start.2 = (f32[3,8]{1,0:T(4,128)S(1)}, f32[3,8]{1,0:T(4,128)}, u32[]{:S(2)}) copy-start(f32[3,8]{1,0:T(4,128)} %param.8) | copy-start | bytes 292
  77.2 19.3 %all-to-all-start.1 = ((bf16[8,2,14336]{2,1,0:T(2,128)(2,1)}), bf16[8,2,14336]{2,1,0:T(2,128)(2,1)S(1)}, u32[]{:S(2)}, u32[]{:S(2)}) async-start(bf16[8,2,14336]{2,1,0:T(2,128)(2,1)} %reshape.97), calls=%async_computation.1 | async-start | bytes 917504 | tf_op jit(solution)/shard_map/all_to_all | solution.py:54
Sparse Core Ops, SparseCore 0:
  47.7 16.6 all-reduce.1
